TPU v7x, 32 devices: a whole 2x2x4 slice. The times are simulated.
32 devices in a mesh: sfc: 8 (over z, core), lev: 4 (over y, x).
Axes of the slice: x: 2, y: 2, z: 4, core: 2. Of those that a mesh axis runs over, the one named last changes fastest.
Arguments:
- tracer_old: float32 [4, 10, 16, 3072], P('lev', None, None, 'sfc'), may hold values from 0.1 to 2
- air_old: float32 [4, 16, 3072], P('lev', None, 'sfc'), may hold values from 0.3 to 20, as said below
- air_new: float32 [4, 16, 3072], P('lev', None, 'sfc'), may hold values from 0.4 to 20, as said below
- dep_coord: float32 [2, 4, 16, 3072], P(None, 'lev', None, 'sfc'), may hold values from -1 to 1
- dep_slot: int32 [4, 16, 3072], P('lev', None, 'sfc'), may hold values from 0 to 639
- fetch_list: int32 [8, 2, 128], P('sfc'), may hold values from 0 to 383, as said below
Outputs:
- tracer_new: float32 [4, 10, 16, 3072], P('lev', None, None, 'sfc')
Inputs may be any that keep to these rules, and one draw needn't show every extreme that they name: `fetch_list`: side 0 holds distinct indices in [128, 384); side 1 holds distinct indices in [0, 256). `air_old`: positive. `air_new`: positive.
All inputs are finite; a program needn't handle non-finite values.
Results may differ from a plain program's by a relative error of at most 0.0003.
Values sent between devices are 32-bit elements; how exact they have to be, the bound alone decides.
A program may use at most 64 MiB of HBM per device.

v0:
```python
import jax
import jax.numpy as jnp
from jax import lax
from jax.sharding import PartitionSpec as P

BAND = 256
NODES = (-1.0, -0.4472135954999579, 0.4472135954999579, 1.0)


def padded(block, sides, width):
    for axis, dim in sides:
        count = lax.axis_size(axis)
        forward = [(i, i + 1) for i in range(count - 1)]
        forward.append((count - 1, 0))
        backward = [(target, source) for source, target in forward]
        low = lax.ppermute(
            lax.slice_in_dim(block, block.shape[dim] - width, None, axis=dim), axis, forward
        )
        high = lax.ppermute(lax.slice_in_dim(block, 0, width, axis=dim), axis, backward)
        block = jnp.concatenate([low, block, high], axis=dim)
    return block


def basis(coord):
    terms = []
    for first in range(4):
        term = jnp.ones_like(coord)
        for other in range(4):
            if other != first:
                term = term * (coord - NODES[other]) / (NODES[first] - NODES[other])
        terms.append(term)
    return terms


def pick_rows(table, slots):
    return table[slots]


def on_device(tracer_old, air_old, air_new, dep_coord, dep_slot, fetch_list):
    e_dev = tracer_old.shape[3]
    levels = tracer_old.shape[0]
    tracers = tracer_old.shape[1]
    points = tracer_old.shape[2]
    old_term = jnp.sum(air_old[:, None] * tracer_old, axis=(0, 2, 3))
    old_mass = lax.psum(old_term, ("sfc", "lev"))
    extended = padded(tracer_old, (("sfc", 3),), BAND)
    left = jnp.take(extended, fetch_list[0, 0] - (e_dev - BAND), axis=3)
    right = jnp.take(extended, BAND + e_dev + fetch_list[0, 1], axis=3)
    buffer = jnp.concatenate([tracer_old, left, right], axis=3)
    width = buffer.shape[3]
    rows = jnp.transpose(buffer, (0, 3, 1, 2)).reshape(levels, width, tracers * points)
    picked = jax.vmap(pick_rows)(rows, dep_slot)
    picked = picked.reshape(levels, points, e_dev, tracers, 16)
    along_a = basis(dep_coord[0])
    along_b = basis(dep_coord[1])
    stacked = jnp.stack([along_a[j // 4] * along_b[j % 4] for j in range(16)], axis=-1)
    interp = jnp.sum(picked * stacked[:, :, :, None, :], axis=-1)
    low = jnp.min(picked, axis=-1)
    high = jnp.max(picked, axis=-1)
    interp = jnp.transpose(interp, (0, 3, 1, 2))
    low = jnp.transpose(low, (0, 3, 1, 2))
    high = jnp.transpose(high, (0, 3, 1, 2))
    clipped = jnp.clip(interp, low, high)
    mass_new = air_new[:, None]
    clip_term = jnp.sum(mass_new * clipped, axis=(0, 2, 3))
    up_term = jnp.sum(mass_new * (high - clipped), axis=(0, 2, 3))
    down_term = jnp.sum(mass_new * (clipped - low), axis=(0, 2, 3))
    summed = lax.psum(jnp.stack([clip_term, up_term, down_term]), ("sfc", "lev"))
    clip_mass = summed[0]
    room_up = summed[1]
    room_down = summed[2]
    shortfall = (old_mass - clip_mass)[None, :, None, None]
    raised = shortfall * (high - clipped) / room_up[None, :, None, None]
    lowered = shortfall * (clipped - low) / room_down[None, :, None, None]
    return clipped + jnp.where(shortfall >= 0, raised, lowered)


def solution(mesh):
    return jax.shard_map(
        on_device,
        mesh=mesh,
        in_specs=(
            P("lev", None, None, "sfc"),
            P("lev", None, "sfc"),
            P("lev", None, "sfc"),
            P(None, "lev", None, "sfc"),
            P("lev", None, "sfc"),
            P("sfc", None, None),
        ),
        out_specs=P("lev", None, None, "sfc"),
        check_vma=False,
    )
```

profile of v0, /device:TPU:0, one launch (start us, length us, event | category | flops | bytes accessed | tf_op | source)
XLA Modules:
  0.0 146.1 jit_solution(4293965998876197416)
XLA Ops:
  0.0 1.0 fusion.7
  1.6 4.1 %collective-permute-start.1 = (f32[1,10,16,256]{3,2,1,0:T(8,128)S(1)}, f32[1,10,16,256]{3,2,1,0:T(8,128)S(1)}, u32[]{:S(2)}, u32[]{:S(2)}) collective-permute-start(f32[1,10,16,256]{3,2,1,0:T(8,128)S(1)} %get-tuple-element.22), channel_id=1, source_target_pairs={{4,0},{8,4},{12,8},{16,12},{20,16},{24,20},{28,24},{0,28},{5,1},{9... | collective-permute-start | bytes 491528 | tf_op jit(solution)/shard_map/ppermute | solution.py:19
  7.2 0.8 constant_dynamic-update-slice_fusion.15
  8.8 0.8 constant_dynamic-update-slice_fusion.13
  9.5 0.8 constant_dynamic-update-slice_fusion.12
  10.3 0.8 constant_dynamic-update-slice_fusion.11
  12.7 0.8 constant_dynamic-update-slice_fusion.8
  13.4 0.8 constant_dynamic-update-slice_fusion.7
  15.8 0.8 constant_dynamic-update-slice_fusion.4
  16.5 0.8 constant_dynamic-update-slice_fusion.3
  17.3 0.8 constant_dynamic-update-slice_fusion.2
  18.1 0.8 constant_dynamic-update-slice_fusion.1
  18.9 0.8 constant_dynamic-update-slice_fusion
  20.4 1.1 multiply_reduce_fusion.4
  21.5 1.0 pad_maximum_fusion
  22.5 5.8 %copy.16 = f32[1,10,16,896]{2,1,3,0:T(8,128)} copy(f32[1,10,16,896]{3,2,1,0:T(8,128)S(1)} %pad_maximum_fusion) | data formatting | bytes 1146880 | tf_op jit(solution)/shard_map/concatenate | solution.py:20
  28.4 3.8 %gather_fusion.1 = f32[128,10,16]{2,1,0:T(8,128)S(1)} fusion(f32[10,16,896]{1,0,2:T(8,128)} %bitcast.103, s32[1024]{0:T(1024)S(1)} %pad_clamp_fusion.1), kind=kCustom, calls=%fused_computation.clone | custom fusion | bytes 164352 | tf_op jit(solution)/shard_map/jit(_take)/gather | solution.py:47
  32.1 4.7 %gather_fusion.2 = f32[128,10,16]{2,1,0:T(8,128)} fusion(f32[10,16,896]{1,0,2:T(8,128)} %bitcast.104, s32[1024]{0:T(1024)S(1)} %pad_clamp_fusion), kind=kCustom, calls=%fused_computation.1.clone | custom fusion | bytes 164352 | tf_op jit(solution)/shard_map/jit(_take)/gather | solution.py:48
  36.8 1.6 %bitcast_select_fusion = (f32[1,10,16,128]{2,1,3,0:T(8,128)S(1)}, f32[1,10,16,128]{2,1,3,0:T(8,128)S(1)}) fusion(f32[128,10,16]{2,1,0:T(8,128)} %gather_fusion.2, pred[128]{0:T(512)(128)(4,1)S(1)} %get-tuple-element.25, f32[128,10,16]{2,1,0:T(8,128)S(1)} %gather_fusion.1, pred[128]{0:T(512)(128)(4,1)S(1)} %get-tuple-element.17), kind=kLoop, calls=%fused_computation.4 | loop fusion | flops 40960 | bytes 327936 | tf_op jit(solution)/shard_map/jit(_take)/select_n | solution.py:48
  39.3 57.0 %gather_fusion = f32[6144,160]{1,0:T(8,128)} fusion(f32[1,640,160]{2,1,0:T(8,128)S(1)} %copy.20, s32[6144]{0:T(1024)S(1)} %reshape.935), kind=kCustom, calls=%fused_computation.2 | custom fusion | bytes 7913472 | tf_op jit(solution)/shard_map/vmap()/gather | solution.py:36
  96.3 6.0 %copy.21 = f32[6144,160]{0,1:T(8,128)} copy(f32[6144,160]{1,0:T(8,128)} %gather_fusion) | data formatting | bytes 7864320 | tf_op jit(solution)/shard_map/vmap()/gather | solution.py:36
  102.2 2.9 %copy.22 = f32[20,8,16,384]{3,2,1,0:T(8,128)S(1)} copy(f32[20,8,16,384]{3,1,2,0:T(8,128)} %bitcast.102) | data formatting | bytes 7864320
  106.1 39.2 %all-reduce = (f32[3,10]{1,0:T(4,128)S(1)}, f32[10]{0:T(128)S(1)}) all-reduce(f32[3,10]{1,0:T(4,128)S(1)} %pad_maximum_fusion.2, f32[10]{0:T(128)S(1)} %multiply_reduce_fusion.4), channel_id=1, replica_groups=mesh['sfc'=8,'lev'=4] {'sfc','lev'}, use_global_device_ids=true, to_apply=%region_8.10 | all-reduce | flops 40 | bytes 320 | tf_op jit(solution)/shard_map/psum | solution.py:68
  145.2 0.9 select_add_fusion
  (32 shorter events, 8.5 us)
Async XLA Ops:
  1.0 20.5 %collective-permute-start = (f32[1,10,16,256]{3,2,1,0:T(8,128)S(1)}, f32[1,10,16,256]{3,2,1,0:T(8,128)S(1)}, u32[]{:S(2)}, u32[]{:S(2)}) collective-permute-start(f32[1,10,16,256]{3,2,1,0:T(8,128)S(1)} %get-tuple-element.21), channel_id=1, source_target_pairs={{0,4},{4,8},{8,12},{12,16},{16,20},{20,24},{24,28},{28,0},{1,5},{5... | collective-permute-start | bytes 491528 | tf_op jit(solution)/shard_map/ppermute | solution.py:16
  1.6 20.0 %collective-permute-start.1 = (f32[1,10,16,256]{3,2,1,0:T(8,128)S(1)}, f32[1,10,16,256]{3,2,1,0:T(8,128)S(1)}, u32[]{:S(2)}, u32[]{:S(2)}) collective-permute-start(f32[1,10,16,256]{3,2,1,0:T(8,128)S(1)} %get-tuple-element.22), channel_id=1, source_target_pairs={{4,0},{8,4},{12,8},{16,12},{20,16},{24,20},{28,24},{0,28},{5,1},{9... | collective-permute-start | bytes 491528 | tf_op jit(solution)/shard_map/ppermute | solution.py:19
  19.7 0.7 copy-start.1
  28.4 10.6 %copy-start = (f32[1,10,16,384]{3,2,1,0:T(8,128)S(1)}, f32[1,10,16,384]{3,2,1,0:T(8,128)}, u32[]{:S(2)}) copy-start(f32[1,10,16,384]{3,2,1,0:T(8,128)} %param.8) | copy-start | bytes 737284
  102.2 2.9 %copy-start.2 = (f32[1,16,384,16]{2,1,3,0:T(8,128)S(1)}, f32[1,16,384,16]{2,1,3,0:T(8,128)}, u32[]{:S(2)}) copy-start(f32[1,16,384,16]{2,1,3,0:T(8,128)} %copy-done.1) | copy-start | bytes 1179652
  105.1 0.7 copy-start.3
where the time goes:
time: 148 us; the launch traced here: 146 us
  local copies, waits for them, and re-layouts  82.9 us (56%)
  blocking collectives  39.2 us (26%)
  other arithmetic  19.3 us (13%)
  starting transfers between devices  4.64 us (3%)
    gather x4, local copies, waits for them, and re-layouts, pick_rows(): return table[slots]  63 us
    psum x1, blocking collectives, on_device(): lax.psum(jnp.stack([clip_term, up_term, down_term]), ('sfc', 'lev'))  39.2 us
    unnamed x15, other arithmetic  11.7 us
    concatenate x1, local copies, waits for them, and re-layouts, padded(): block = jnp.concatenate([low, block, high], axis=dim)  5.84 us
    gather x1, local copies, waits for them, and re-layouts, on_device(): right = jnp.take(extended, BAND + e_dev + fetch_list[0, 1], axis=3)  4.7 us
    ppermute x1, starting transfers between devices, padded(): lax.ppermute(lax.slice_in_dim(block, 0, width, axis=dim), axis, backward)  4.09 us
    unnamed x9, local copies, waits for them, and re-layouts  3.77 us
    gather x1, local copies, waits for them, and re-layouts, on_device(): left = jnp.take(extended, fetch_list[0, 0] - (e_dev - BAND), axis=3)  3.77 us
  transfers between devices with their start and end apart: 2, of which 0 were waited for; matrix products, arithmetic and copies ran while one was open for 10% of the time, Pallas kernels for 0%

commit v1 on v0

--- a/solution.py
+++ b/solution.py
@@ -65,7 +65,8 @@
     clip_term = jnp.sum(mass_new * clipped, axis=(0, 2, 3))
     up_term = jnp.sum(mass_new * (high - clipped), axis=(0, 2, 3))
     down_term = jnp.sum(mass_new * (clipped - low), axis=(0, 2, 3))
-    summed = lax.psum(jnp.stack([clip_term, up_term, down_term]), ("sfc", "lev"))
+    one_axis = lax.psum(jnp.stack([clip_term, up_term, down_term]), "lev")
+    summed = lax.psum(one_axis, "sfc")
     clip_mass = summed[0]
     room_up = summed[1]
     room_down = summed[2]

time: 148 us -> 181 us (1.22)
  blocking collectives: 39.2 us -> 62.5 us
  other arithmetic: 19.3 us -> 30 us
    psum x1 -> x3, blocking collectives: 39.2 us -> 62.5 us  [the longest x1 39.2 us: on_device(): old_mass = lax.psum(old_term, ('sfc', 'lev'))]
    unnamed x15, other arithmetic: 11.7 us -> 20.7 us
    unnamed x9 -> x5, local copies, waits for them, and re-layouts: 3.77 us -> 2.81 us
  transfers between devices with their start and end apart: 2 -> 2, of which waited for: 0 -> 0; matrix products, arithmetic and copies ran while one was open for 10% -> 14% of each run, Pallas kernels for 0% -> 0%
where the time goes in v1:
time: 181 us; the launch traced here: 179 us
  local copies, waits for them, and re-layouts  81.9 us (45%)
  blocking collectives  62.5 us (35%)
  other arithmetic  30 us (17%)
  starting transfers between devices  4.64 us (3%)
    gather x4, local copies, waits for them, and re-layouts, pick_rows(): return table[slots]  63 us
    psum x1, blocking collectives, on_device(): old_mass = lax.psum(old_term, ('sfc', 'lev'))  39.2 us
    unnamed x15, other arithmetic  20.7 us
    psum x1, blocking collectives, on_device(): summed = lax.psum(one_axis, 'sfc')  13.6 us
    psum x1, blocking collectives, on_device(): one_axis = lax.psum(jnp.stack([clip_term, up_term, down_term]), 'lev')  9.74 us
    concatenate x1, local copies, waits for them, and re-layouts, padded(): block = jnp.concatenate([low, block, high], axis=dim)  5.84 us
    gather x1, local copies, waits for them, and re-layouts, on_device(): right = jnp.take(extended, BAND + e_dev + fetch_list[0, 1], axis=3)  4.7 us
    ppermute x1, starting transfers between devices, padded(): lax.ppermute(lax.slice_in_dim(block, 0, width, axis=dim), axis, backward)  4.09 us
  transfers between devices with their start and end apart: 2, of which 0 were waited for; matrix products, arithmetic and copies ran while one was open for 14% of the time, Pallas kernels for 0%

profile of v1, /device:TPU:0, one launch (start us, length us, event | category | flops | bytes accessed | tf_op | source)
XLA Modules:
  0.0 179.1 jit_solution(1257627007938516442)
XLA Ops:
  1.6 4.1 %collective-permute-start.1 = (f32[1,10,16,256]{3,2,1,0:T(8,128)S(1)}, f32[1,10,16,256]{3,2,1,0:T(8,128)S(1)}, u32[]{:S(2)}, u32[]{:S(2)}) collective-permute-start(f32[1,10,16,256]{3,2,1,0:T(8,128)S(1)} %get-tuple-element.20), channel_id=1, source_target_pairs={{4,0},{8,4},{12,8},{16,12},{20,16},{24,20},{28,24},{0,28},{5,1},{9... | collective-permute-start | bytes 491528 | tf_op jit(solution)/shard_map/ppermute | solution.py:19
  8.6 1.4 constant_dynamic-update-slice_fusion.14
  9.9 1.4 constant_dynamic-update-slice_fusion.13
  11.3 1.4 constant_dynamic-update-slice_fusion.12
  12.7 1.4 constant_dynamic-update-slice_fusion.11
  14.1 1.4 constant_dynamic-update-slice_fusion.10
  15.5 1.4 constant_dynamic-update-slice_fusion.9
  16.9 1.4 constant_dynamic-update-slice_fusion.8
  18.2 1.4 constant_dynamic-update-slice_fusion.7
  19.6 1.4 constant_dynamic-update-slice_fusion.6
  21.0 1.4 constant_dynamic-update-slice_fusion.5
  25.1 1.4 constant_dynamic-update-slice_fusion.2
  27.9 1.4 constant_dynamic-update-slice_fusion
  30.3 39.2 %psum.21 = f32[10]{0:T(128)S(1)} all-reduce(f32[10]{0:T(128)S(1)} %multiply_reduce_fusion.4), channel_id=1, replica_groups=mesh['sfc'=8,'lev'=4] {'sfc','lev'}, use_global_device_ids=true, to_apply=%region_4.6 | all-reduce | flops 10 | bytes 80 | tf_op jit(solution)/shard_map/psum | solution.py:45
  70.5 5.8 %copy.16 = f32[1,10,16,896]{2,1,3,0:T(8,128)} copy(f32[1,10,16,896]{3,2,1,0:T(8,128)S(1)} %pad_maximum_fusion) | data formatting | bytes 1146880 | tf_op jit(solution)/shard_map/concatenate | solution.py:20
  76.4 3.8 %gather_fusion.1 = f32[128,10,16]{2,1,0:T(8,128)S(1)} fusion(f32[10,16,896]{1,0,2:T(8,128)} %bitcast.103, s32[1024]{0:T(1024)S(1)} %pad_clamp_fusion.1), kind=kCustom, calls=%fused_computation.clone | custom fusion | bytes 164352 | tf_op jit(solution)/shard_map/jit(_take)/gather | solution.py:47
  80.1 4.7 %gather_fusion.2 = f32[128,10,16]{2,1,0:T(8,128)} fusion(f32[10,16,896]{1,0,2:T(8,128)} %bitcast.104, s32[1024]{0:T(1024)S(1)} %pad_clamp_fusion), kind=kCustom, calls=%fused_computation.1.clone | custom fusion | bytes 164352 | tf_op jit(solution)/shard_map/jit(_take)/gather | solution.py:48
  84.9 1.6 bitcast_select_fusion
  87.3 57.0 %gather_fusion = f32[6144,160]{1,0:T(8,128)} fusion(f32[1,640,160]{2,1,0:T(8,128)S(1)} %copy.20, s32[6144]{0:T(1024)S(1)} %reshape.935), kind=kCustom, calls=%fused_computation.2 | custom fusion | bytes 7913472 | tf_op jit(solution)/shard_map/vmap()/gather | solution.py:36
  144.3 6.0 %copy.21 = f32[6144,160]{0,1:T(8,128)} copy(f32[6144,160]{1,0:T(8,128)} %gather_fusion) | data formatting | bytes 7864320 | tf_op jit(solution)/shard_map/vmap()/gather | solution.py:36
  150.3 2.8 %copy.22 = f32[20,8,16,384]{3,2,1,0:T(8,128)S(1)} copy(f32[20,8,16,384]{3,1,2,0:T(8,128)} %bitcast.102) | data formatting | bytes 7864320
  153.1 1.6 fusion.5
  154.9 9.7 %psum.22 = f32[3,10]{1,0:T(4,128)S(1)} all-reduce(f32[3,10]{1,0:T(4,128)S(1)} %pad_maximum_fusion.2), channel_id=1, replica_groups=mesh['sfc'=8,'lev'=4] {'lev'}, use_global_device_ids=true, to_apply=%region_8.10 | all-reduce | flops 30 | bytes 240 | tf_op jit(solution)/shard_map/psum | solution.py:68
  164.7 13.6 %psum.23 = f32[3,10]{1,0:T(4,128)S(1)} all-reduce(f32[3,10]{1,0:T(4,128)S(1)} %psum.22), channel_id=1, replica_groups=mesh['sfc'=8,'lev'=4] {'sfc'}, use_global_device_ids=true, to_apply=%region_9.11 | all-reduce | flops 30 | bytes 240 | tf_op jit(solution)/shard_map/psum | solution.py:69
  (30 shorter events, 12.6 us)
Async XLA Ops:
  1.0 68.5 %collective-permute-start = (f32[1,10,16,256]{3,2,1,0:T(8,128)S(1)}, f32[1,10,16,256]{3,2,1,0:T(8,128)S(1)}, u32[]{:S(2)}, u32[]{:S(2)}) collective-permute-start(f32[1,10,16,256]{3,2,1,0:T(8,128)S(1)} %get-tuple-element.19), channel_id=1, source_target_pairs={{0,4},{4,8},{8,12},{12,16},{16,20},{20,24},{24,28},{28,0},{1,5},{5... | collective-permute-start | bytes 491528 | tf_op jit(solution)/shard_map/ppermute | solution.py:16
  1.6 68.0 %collective-permute-start.1 = (f32[1,10,16,256]{3,2,1,0:T(8,128)S(1)}, f32[1,10,16,256]{3,2,1,0:T(8,128)S(1)}, u32[]{:S(2)}, u32[]{:S(2)}) collective-permute-start(f32[1,10,16,256]{3,2,1,0:T(8,128)S(1)} %get-tuple-element.20), channel_id=1, source_target_pairs={{4,0},{8,4},{12,8},{16,12},{20,16},{24,20},{28,24},{0,28},{5,1},{9... | collective-permute-start | bytes 491528 | tf_op jit(solution)/shard_map/ppermute | solution.py:19
  76.4 10.6 %copy-start = (f32[1,10,16,384]{3,2,1,0:T(8,128)S(1)}, f32[1,10,16,384]{3,2,1,0:T(8,128)}, u32[]{:S(2)}) copy-start(f32[1,10,16,384]{3,2,1,0:T(8,128)} %param.8) | copy-start | bytes 737284
  153.1 1.6 copy-start.1
